TPU v7x, 32 devices: a whole 2x2x4 slice. The times are simulated.
32 devices in a mesh: energy: 8 (over z, y), slab: 4 (over x, core).
Axes of the slice: x: 2, y: 2, z: 4, core: 2. Of those that a mesh axis runs over, the one named last changes fastest.
Arguments:
- green_blocks: bfloat16 [16, 4, 512, 512], P('energy', 'slab'), may hold values from -6 to 6
- coupling: bfloat16 [4, 512, 512], P('slab'), may hold values from -0.25 to 0.25
- coulomb: bfloat16 [4, 512, 512], P('slab'), may hold values from -0.25 to 0.25
Outputs:
- self_energy: bfloat16 [16, 4, 512, 512], P('energy', 'slab')
- screening: bfloat16 [16, 4, 512, 512], P('energy', 'slab')
All inputs are finite; a program needn't handle non-finite values.
Results may differ from a plain program's by a relative error of at most 0.0075.
Values may be sent and summed in bfloat16 or wider, within the bound.
A program may use at most 64 MiB of HBM per device.

v0:
```python
import functools

import jax
import jax.numpy as jnp
from jax import lax
from jax.experimental import pallas as pl
from jax.experimental.pallas import tpu as pltpu
from jax.sharding import PartitionSpec as P

MESH = pl.DeviceIdType.MESH
F32, BF16 = jnp.float32, jnp.bfloat16
TILE = 16
LANES = 128


def matmul(a, b, a_dim=1, b_dim=0):
    return lax.dot_general(a, b, (((a_dim,), (b_dim,)), ((), ())), preferred_element_type=F32)


def correlate(gath, prow, row0, rows):
    count, _, m = gath.shape
    scale = float(count) ** -0.5
    across = m // LANES

    def tile(i, _):
        r = pl.ds(pl.multiple_of(row0 + (i // across) * TILE, TILE), TILE)
        l = pl.ds(pl.multiple_of((i % across) * LANES, LANES), LANES)

        def put(w, total):
            value = (total * scale).astype(BF16)
            prow[w, r, l] = value
            return value

        if count <= 16:
            x = [gath[e, r, l].astype(F32) for e in range(count)]
            for w in range(count // 2 + 1):
                if 2 * w == count:
                    terms = [x[e] * x[e + w] for e in range(w)]
                else:
                    terms = [x[e] * x[(e + w) % count] for e in range(count)]
                while len(terms) > 1:
                    terms = [sum(terms[j : j + 2]) for j in range(0, len(terms), 2)]
                total = terms[0] * 2.0 if 2 * w == count else terms[0]
                value = put(w, total)
                if 0 < w < count - w:
                    prow[count - w, r, l] = value
        else:

            def lag(w, _):
                def term(e, total):
                    return total + gath[e, r, l].astype(F32) * gath[(e + w) % count, r, l].astype(F32)

                put(w, lax.fori_loop(0, count, term, jnp.zeros((TILE, LANES), F32)))
                return 0

            lax.fori_loop(0, count, lag, 0)
        return 0

    lax.fori_loop(0, (rows // TILE) * across, tile, 0)


def kernel(
    n, ns, parts, green, coupling, coulomb, sigma, screen,
    g, h, c, gath, prow, pol, inner, rim_b, rim_a, g_above, low_in, low_out, outer,
    local, ss1, rs1, ss2, rs2, ssb, rsb, ssa, rsa, sside, rside,
):
    per, m = g.shape[0], g.shape[1]
    rows = m // n // parts
    me, slab = lax.axis_index("energy"), lax.axis_index("slab")
    up, down = jnp.minimum(slab + 1, ns - 1), jnp.maximum(slab - 1, 0)
    has_up, has_down = slab < ns - 1, slab > 0
    order = range(1, n)

    def partner(i):
        other, bit = me, 1
        while bit <= i:
            if i & bit:
                other = other + bit * (1 - 2 * (me // bit % 2))
            bit *= 2
        return other


    def block(part, owner):
        return pl.ds(pl.multiple_of(part * (m // parts) + owner * rows, rows), rows)

    loads = [
        pltpu.make_async_copy(green.at[:, 0], g, local.at[0]),
        pltpu.make_async_copy(coupling.at[0], h, local.at[1]),
        pltpu.make_async_copy(coulomb.at[0], c, local.at[2]),
    ]
    own = [
        pltpu.make_async_copy(
            green.at[:, 0, block(part, me)],
            gath.at[pl.ds(me * per, per), pl.ds(part * rows, rows)],
            local.at[3 + part],
        )
        for part in range(parts)
    ]
    for copy in loads + own:
        copy.start()

    barrier = pltpu.get_barrier_semaphore()
    for i in range(1, n):
        pl.semaphore_signal(barrier, inc=1, device_id={"energy": (me + i) % n}, device_id_type=MESH)

    @pl.when(has_up)
    def _():
        pl.semaphore_signal(barrier, inc=1, device_id={"slab": up}, device_id_type=MESH)

    @pl.when(has_down)
    def _():
        pl.semaphore_signal(barrier, inc=1, device_id={"slab": down}, device_id_type=MESH)

    pl.semaphore_wait(barrier, n - 1 + has_up.astype(jnp.int32) + has_down.astype(jnp.int32))

    def remote(src, dst, send, recv, where):
        return pltpu.make_async_remote_copy(
            src_ref=src, dst_ref=dst, send_sem=send, recv_sem=recv, device_id=where, device_id_type=MESH
        )

    loads[0].wait()
    first = {}
    for part in range(parts):
        for i in order:
            to = partner(i)
            first[part, i] = remote(
                g.at[:, block(part, to)],
                gath.at[pl.ds(me * per, per), pl.ds(part * rows, rows)],
                ss1.at[part, i], rs1.at[part, i], {"energy": to},
            )
            first[part, i].start()

    green_down = remote(g, g_above, sside.at[0], rside.at[0], {"slab": down})
    lower_up = remote(low_out, low_in, sside.at[1], rside.at[1], {"slab": up})

    @pl.when(has_down)
    def _():
        green_down.start()

    @pl.when(jnp.logical_not(has_down))
    def _():
        low_in[...] = jnp.zeros_like(low_in)
        rim_b[...] = jnp.zeros_like(rim_b)

    loads[1].wait()

    def lower(e, _):
        mid = matmul(g[e], h[...]).astype(BF16)
        low_out[e] = matmul(h[...], mid, 0, 0).astype(BF16)
        return 0

    lax.fori_loop(0, per, lower, 0)

    @pl.when(jnp.logical_not(has_up))
    def _():
        g_above[...] = jnp.zeros_like(g_above)
        rim_a[...] = jnp.zeros_like(rim_a)

    @pl.when(has_up)
    def _():
        lower_up.start()

    def self_energy():
        @pl.when(has_up)
        def _():
            green_down.wait_recv()

        @pl.when(has_down)
        def _():
            lower_up.wait_recv()

        def upper(e, _):
            mid = matmul(g_above[e], h[...], 1, 1).astype(BF16)
            term = matmul(h[...], mid).astype(BF16)
            sigma[e, 0] = (low_in[e].astype(F32) + term.astype(F32)).astype(BF16)
            return 0

        lax.fori_loop(0, per, upper, 0)

    second, rims = {}, {}

    def forward(part, i):
        piece = block(part, partner(i))
        rims[part, i] = (
            remote(pol.at[:, piece], rim_b.at[:, piece], ssb.at[part, i], rsb.at[part, i], {"slab": up}),
            remote(pol.at[:, piece], rim_a.at[:, piece], ssa.at[part, i], rsa.at[part, i], {"slab": down}),
        )

        @pl.when(has_up)
        def _():
            rims[part, i][0].start()

        @pl.when(has_down)
        def _():
            rims[part, i][1].start()

    for part in range(parts):
        own[part].wait()
        for i in order:
            first[part, i].wait_recv()
        correlate(gath, prow, part * rows, rows)
        span = pl.ds(part * rows, rows)
        pol[:, block(part, me)] = prow[pl.ds(me * per, per), span]
        for i in order:
            to = partner(i)
            second[part, i] = remote(
                prow.at[pl.ds(to * per, per), span], pol.at[:, block(part, me)],
                ss2.at[part, i], rs2.at[part, i], {"energy": to},
            )
            second[part, i].start()
        forward(part, 0)
        if part == 0:
            self_energy()

    loads[2].wait()
    for part in range(parts):
        for i in order:
            second[part, i].wait_recv()
            forward(part, i)
        half = pl.ds(part * (m // parts), m // parts)

        def screen_inner(e, _):
            inner[e, half] = matmul(pol[e, half], c[...], 1, 1).astype(BF16)
            return 0

        lax.fori_loop(0, per, screen_inner, 0)

    def screen_outer(e, _):
        outer[e] = matmul(c[...], inner[e])
        return 0

    lax.fori_loop(0, per, screen_outer, 0)

    for part in range(parts):
        for i in range(n):
            @pl.when(has_down)
            def _():
                rims[part, i][0].wait_recv()

            @pl.when(has_up)
            def _():
                rims[part, i][1].wait_recv()

        half = pl.ds(part * (m // parts), m // parts)
        for e in range(per):
            beside = rim_b[e, half].astype(F32) + rim_a[e, half].astype(F32)
            screen[e, 0, half] = (outer[e, half] + 0.5 * beside).astype(BF16)

    for copy in list(first.values()) + list(second.values()):
        copy.wait_send()

    @pl.when(has_up)
    def _():
        lower_up.wait_send()
        for copies in rims.values():
            copies[0].wait_send()

    @pl.when(has_down)
    def _():
        green_down.wait_send()
        for copies in rims.values():
            copies[1].wait_send()


def store(sigma, screen, sigma_out, screen_out, sems):
    copies = [
        pltpu.make_async_copy(sigma, sigma_out, sems.at[0]),
        pltpu.make_async_copy(screen, screen_out, sems.at[1]),
    ]
    for copy in copies:
        copy.start()
    for copy in copies:
        copy.wait()


def solution(mesh):
    n, ns = mesh.shape["energy"], mesh.shape["slab"]
    assert n & (n - 1) == 0

    def step(green, coupling, coulomb):
        per, m, count = green.shape[0], green.shape[-1], green.shape[0] * n
        parts = max(k for k in (1, 2) if m // n % (k * TILE) == 0)
        rows = m // n
        blocks = pltpu.VMEM((per, m, m), BF16)
        square = pltpu.VMEM((m, m), BF16)
        strip = pltpu.VMEM((count, rows, m), BF16)
        sems = pltpu.SemaphoreType.DMA((parts, n))
        shapes = [jax.ShapeDtypeStruct(green.shape, BF16)] * 2
        near = pl.BlockSpec(memory_space=pltpu.VMEM)
        far = pl.BlockSpec(memory_space=pltpu.HBM)
        held = pl.pallas_call(
            functools.partial(kernel, n, ns, parts),
            out_shape=shapes,
            in_specs=[far] * 3,
            out_specs=[near] * 2,
            scratch_shapes=[blocks, square, square, strip, strip]
            + [blocks] * 6
            + [blocks, pltpu.VMEM((per, m, m), F32)]
            + [pltpu.SemaphoreType.DMA((3 + parts,))]
            + [sems] * 8
            + [pltpu.SemaphoreType.DMA((2,))] * 2,
            compiler_params=pltpu.CompilerParams(
                collective_id=0, has_side_effects=True, vmem_limit_bytes=40 * 1024 * 1024
            ),
            name="step",
        )(*(pltpu.with_memory_space_constraint(x, pltpu.HBM) for x in (green, coupling, coulomb)))
        return tuple(
            pl.pallas_call(
                store,
                out_shape=shapes,
                in_specs=[near] * 2,
                out_specs=[far] * 2,
                scratch_shapes=[pltpu.SemaphoreType.DMA((2,))],
                compiler_params=pltpu.CompilerParams(vmem_limit_bytes=8 * 1024 * 1024),
                name="store",
            )(*held)
        )

    placed = (P("energy", "slab", None, None), P("slab", None, None), P("slab", None, None))
    return jax.shard_map(
        step,
        mesh=mesh,
        in_specs=placed,
        out_specs=(P("energy", "slab", None, None),) * 2,
        check_vma=False,
    )
```

profile of v0, /device:TPU:1, one launch (start us, length us, event | category | flops | bytes accessed | tf_op | source)
XLA Modules:
  0.0 58.5 jit_solution(842265810306560317)
XLA Ops:
  0.6 56.5 %step.1 = (bf16[2,1,512,512]{3,2,1,0:T(8,128)(2,1)S(1)}, bf16[2,1,512,512]{3,2,1,0:T(8,128)(2,1)S(1)}) custom-call(bf16[2,1,512,512]{3,2,1,0:T(8,128)(2,1)} %green.1, bf16[1,512,512]{2,1,0:T(8,128)(2,1)} %coupling.1, bf16[1,512,512]{2,1,0:T(8,128)(2,1)} %coulomb.1), custom_call_target="tpu_custom_call" | custom-call | tf_op jit(solution)/shard_map/step/pallas_call | solution.py:291
  57.1 1.3 %store.1 = (bf16[2,1,512,512]{3,2,1,0:T(8,128)(2,1)}, bf16[2,1,512,512]{3,2,1,0:T(8,128)(2,1)}) custom-call(bf16[2,1,512,512]{3,2,1,0:T(8,128)(2,1)S(1)} %get-tuple-element.4.sigma, bf16[2,1,512,512]{3,2,1,0:T(8,128)(2,1)S(1)} %get-tuple-element.5.screen), custom_call_target="tpu_custom_call" | custom-call | tf_op jit(solution)/shard_map/store/pallas_call | solution.py:308
where the time goes:
time: 58.6 us; the launch traced here: 58.5 us
  Pallas kernels  57.8 us (99%)
  between operations  0.64 us (1%)
    pallas_call x1, Pallas kernels, step(): pl.pallas_call(functools.partial(kernel, n, ns, parts), out_shape=shapes,...  56.5 us
    pallas_call x1, Pallas kernels, step(): pl.pallas_call(store, out_shape=shapes, in_specs=[near] * 2, out_specs=[f...  1.33 us

commit v1 on v0

v1 whole, which is shorter than its diff:
```python
import functools

import jax
import jax.numpy as jnp
from jax import lax
from jax.experimental import pallas as pl
from jax.experimental.pallas import tpu as pltpu
from jax.sharding import PartitionSpec as P

MESH = pl.DeviceIdType.MESH
F32, BF16 = jnp.float32, jnp.bfloat16
TILE = 16
LANES = 128


def matmul(a, b, a_dim=1, b_dim=0):
    return lax.dot_general(a, b, (((a_dim,), (b_dim,)), ((), ())), preferred_element_type=F32)


def correlate(gath, prow, row0, rows):
    count, _, m = gath.shape
    scale = float(count) ** -0.5
    across = m // LANES

    def tile(i, _):
        r = pl.ds(pl.multiple_of(row0 + (i // across) * TILE, TILE), TILE)
        l = pl.ds(pl.multiple_of((i % across) * LANES, LANES), LANES)

        def put(w, total):
            value = (total * scale).astype(BF16)
            prow[w, r, l] = value
            return value

        if count <= 16:
            x = [gath[e, r, l].astype(F32) for e in range(count)]
            for w in range(count // 2 + 1):
                if 2 * w == count:
                    terms = [x[e] * x[e + w] for e in range(w)]
                else:
                    terms = [x[e] * x[(e + w) % count] for e in range(count)]
                while len(terms) > 1:
                    terms = [sum(terms[j : j + 2]) for j in range(0, len(terms), 2)]
                total = terms[0] * 2.0 if 2 * w == count else terms[0]
                value = put(w, total)
                if 0 < w < count - w:
                    prow[count - w, r, l] = value
        else:

            def lag(w, _):
                def term(e, total):
                    return total + gath[e, r, l].astype(F32) * gath[(e + w) % count, r, l].astype(F32)

                put(w, lax.fori_loop(0, count, term, jnp.zeros((TILE, LANES), F32)))
                return 0

            lax.fori_loop(0, count, lag, 0)
        return 0

    lax.fori_loop(0, (rows // TILE) * across, tile, 0)


def split(rows):
    units, sizes = rows // TILE, []
    while units > 1 and len(sizes) < 1:
        sizes.append(units - units // 2)
        units //= 2
    return [size * TILE for size in sizes + [units]]


def kernel(
    n, ns, sizes, green, coupling, coulomb, sigma, screen,
    g, h, c, gath, prow, pol, inner, rim_b, rim_a, g_above, low_in, low_out, outer,
    local, ss1, rs1, ss2, rs2, ssb, rsb, ssa, rsa, sside, rside, seen,
):
    per, m = g.shape[0], g.shape[1]
    parts, last = range(len(sizes)), len(sizes) - 1
    starts = [sum(sizes[:part]) for part in parts]
    me, slab = lax.axis_index("energy"), lax.axis_index("slab")
    up, down = jnp.minimum(slab + 1, ns - 1), jnp.maximum(slab - 1, 0)
    has_up, has_down = slab < ns - 1, slab > 0
    long = n // 2
    half = max(long // 2, 1)
    z, y = me // 2, me % 2
    low = z < half
    base = jnp.where(low, 0, half)

    def pair(place):
        return [place * 2 + y, place * 2 + 1 - y]

    near = [me + 1 - 2 * y]
    for k in range(1, half):
        near += pair(base + (z - base + k) % half)
    cross = []
    for k in range(long - half):
        cross += pair(jnp.where(low, long - 1 - k, k))
    others = near + cross

    def block(part, owner):
        rows = sizes[part]
        return pl.ds(pl.multiple_of(n * starts[part] + owner * rows, TILE), rows)

    def strip(part):
        return pl.ds(starts[part], sizes[part])

    def span(part):
        return pl.ds(n * starts[part], n * sizes[part])

    loads = [
        pltpu.make_async_copy(green.at[:, 0], g, local.at[0]),
        pltpu.make_async_copy(coupling.at[0], h, local.at[1]),
        pltpu.make_async_copy(coulomb.at[0], c, local.at[2]),
    ]
    own = [
        pltpu.make_async_copy(
            green.at[:, 0, block(part, me)],
            gath.at[pl.ds(me * per, per), strip(part)],
            local.at[3 + part],
        )
        for part in parts
    ]
    for copy in loads + own:
        copy.start()

    def remote(src, dst, send, recv, where):
        return pltpu.make_async_remote_copy(
            src_ref=src, dst_ref=dst, send_sem=send, recv_sem=recv, device_id=where, device_id_type=MESH
        )

    def at(steps, flip):
        place = z + steps
        other = jnp.clip(place, 0, long - 1) * 2 + (1 - y if flip else y)
        return other, (place >= 0) & (place < long)

    def ring(distance):
        found = [(distance, 0), (-distance, 0)] if distance < long else []
        found += [(steps, 1) for steps in sorted({distance - 1, 1 - distance}, reverse=True)]
        return [at(*place) for place in found]

    def greet(sem, others):
        count = jnp.int32(0)
        for where, there in others:
            @pl.when(there)
            def _():
                pl.semaphore_signal(sem, inc=1, device_id=where, device_id_type=MESH)

            count = count + there.astype(jnp.int32)
        pl.semaphore_wait(sem, count)

    def gather(part, to):
        return remote(
            g.at[:, block(part, to)],
            gath.at[pl.ds(me * per, per), strip(part)],
            ss1.at[part, to], rs1.at[part, me], {"energy": to},
        )

    def gathered(part, other):
        return remote(
            g.at[:, block(part, other)],
            gath.at[pl.ds(other * per, per), strip(part)],
            ss1.at[part, other], rs1.at[part, other], {"energy": other},
        )

    beside = [({"energy": to}, there) for to, there in ring(1)]
    for distance in range(1, long + 1):
        if distance == 1:
            greet(pltpu.get_barrier_semaphore(), beside + [({"slab": up}, has_up), ({"slab": down}, has_down)])
            loads[0].wait()
        else:
            greet(seen.at[distance - 2], beside)
        for to, there in ring(distance):
            @pl.when(there)
            def _():
                gather(0, to).start()

    for part in parts[1:]:
        for to in others:
            gather(part, to).start()

    green_down = remote(g, g_above, sside.at[0], rside.at[0], {"slab": down})
    lower_up = remote(low_out, low_in, sside.at[1], rside.at[1], {"slab": up})

    @pl.when(has_down)
    def _():
        green_down.start()

    @pl.when(jnp.logical_not(has_down))
    def _():
        low_in[...] = jnp.zeros_like(low_in)
        rim_b[...] = jnp.zeros_like(rim_b)

    loads[1].wait()

    def lower(e, _):
        mid = matmul(g[e], h[...]).astype(BF16)
        low_out[e] = matmul(h[...], mid, 0, 0).astype(BF16)
        return 0

    lax.fori_loop(0, per, lower, 0)

    @pl.when(jnp.logical_not(has_up))
    def _():
        g_above[...] = jnp.zeros_like(g_above)
        rim_a[...] = jnp.zeros_like(rim_a)

    @pl.when(has_up)
    def _():
        lower_up.start()

    def self_energy():
        @pl.when(has_up)
        def _():
            green_down.wait_recv()

        @pl.when(has_down)
        def _():
            lower_up.wait_recv()

        def upper(e, _):
            mid = matmul(g_above[e], h[...], 1, 1).astype(BF16)
            term = matmul(h[...], mid).astype(BF16)
            sigma[e, 0] = (low_in[e].astype(F32) + term.astype(F32)).astype(BF16)
            return 0

        lax.fori_loop(0, per, upper, 0)

    def scatter(part, to):
        return remote(
            prow.at[pl.ds(to * per, per), strip(part)], pol.at[:, block(part, me)],
            ss2.at[part, to], rs2.at[part, me], {"energy": to},
        )

    def scattered(part, other):
        return remote(
            prow.at[pl.ds(other * per, per), strip(part)], pol.at[:, block(part, other)],
            ss2.at[part, other], rs2.at[part, other], {"energy": other},
        )

    def to_up(part, owner):
        piece = block(part, owner)
        return remote(pol.at[:, piece], rim_b.at[:, piece], ssb.at[part, owner], rsb.at[part, owner], {"slab": up})

    def to_down(part, owner):
        piece = block(part, owner)
        return remote(pol.at[:, piece], rim_a.at[:, piece], ssa.at[part, owner], rsa.at[part, owner], {"slab": down})

    def forward(part, owner):
        @pl.when(has_up)
        def _():
            to_up(part, owner).start()

        @pl.when(has_down)
        def _():
            to_down(part, owner).start()

    def arrive(part, owner):
        @pl.when(has_down)
        def _():
            to_up(part, owner).wait_recv()

        @pl.when(has_up)
        def _():
            to_down(part, owner).wait_recv()

    def depart(part):
        @pl.when(has_up)
        def _():
            for owner in [me] + others:
                to_up(part, owner).wait_send()

        @pl.when(has_down)
        def _():
            for owner in [me] + others:
                to_down(part, owner).wait_send()

    def finish(piece):
        for e in range(per):
            sides = rim_b[e, piece].astype(F32) + rim_a[e, piece].astype(F32)
            screen[e, 0, piece] = (outer[e, piece] + 0.5 * sides).astype(BF16)

    def screened(rows, first):
        def product(e, _):
            inner[e, rows] = matmul(pol[e, rows], c[...], 1, 1).astype(BF16)
            term = matmul(c[:, rows], inner[e, rows])
            outer[e] = term if first else outer[e] + term
            return 0

        lax.fori_loop(0, per, product, 0)

    for part in parts:
        own[part].wait()
        for other in others:
            gathered(part, other).wait_recv()
        correlate(gath, prow, starts[part], sizes[part])
        for to in others:
            scatter(part, to).start()
        pol[:, block(part, me)] = prow[pl.ds(me * per, per), strip(part)]
        forward(part, me)
        if part == 0:
            self_energy()

    loads[2].wait()
    for part in parts:
        count = long * sizes[part]
        cut = part == last and n > 2 and n * starts[part] % LANES == count % LANES == 0
        for other in near:
            scattered(part, other).wait_recv()
            forward(part, other)
        if cut:
            side = jnp.where(low, 0, count)
            screened(pl.ds(pl.multiple_of(n * starts[part] + side, LANES), count), part == 0)
        for other in cross:
            scattered(part, other).wait_recv()
            forward(part, other)
        if cut:
            screened(pl.ds(pl.multiple_of(n * starts[part] + count - side, LANES), count), False)
        else:
            screened(span(part), part == 0)

    for part in parts[:last]:
        for owner in [me] + others:
            arrive(part, owner)
        finish(span(part))
        depart(part)
    for part in parts:
        for other in others:
            gathered(part, other).wait_send()
            scattered(part, other).wait_send()

    @pl.when(has_up)
    def _():
        lower_up.wait_send()

    @pl.when(has_down)
    def _():
        green_down.wait_send()

    for owner in [me] + others:
        arrive(last, owner)
        finish(block(last, owner))
    depart(last)


def store(sigma, screen, sigma_out, screen_out, sems):
    copies = [
        pltpu.make_async_copy(sigma, sigma_out, sems.at[0]),
        pltpu.make_async_copy(screen, screen_out, sems.at[1]),
    ]
    for copy in copies:
        copy.start()
    for copy in copies:
        copy.wait()


def solution(mesh):
    n, ns = mesh.shape["energy"], mesh.shape["slab"]
    assert n > 1 and n & (n - 1) == 0

    def step(green, coupling, coulomb):
        per, m, count = green.shape[0], green.shape[-1], green.shape[0] * n
        rows = m // n
        sizes = split(rows)
        parts = len(sizes)
        blocks = pltpu.VMEM((per, m, m), BF16)
        square = pltpu.VMEM((m, m), BF16)
        strip = pltpu.VMEM((count, rows, m), BF16)
        sems = pltpu.SemaphoreType.DMA((parts, n))
        shapes = [jax.ShapeDtypeStruct(green.shape, BF16)] * 2
        near = pl.BlockSpec(memory_space=pltpu.VMEM)
        far = pl.BlockSpec(memory_space=pltpu.HBM)
        held = pl.pallas_call(
            functools.partial(kernel, n, ns, sizes),
            out_shape=shapes,
            in_specs=[far] * 3,
            out_specs=[near] * 2,
            scratch_shapes=[blocks, square, square, strip, strip]
            + [blocks] * 6
            + [blocks, pltpu.VMEM((per, m, m), F32)]
            + [pltpu.SemaphoreType.DMA((3 + parts,))]
            + [sems] * 8
            + [pltpu.SemaphoreType.DMA((2,))] * 2
            + [pltpu.SemaphoreType.REGULAR((max(n // 2 - 1, 1),))],
            compiler_params=pltpu.CompilerParams(
                collective_id=0, has_side_effects=True, vmem_limit_bytes=40 * 1024 * 1024
            ),
            name="step",
        )(*(pltpu.with_memory_space_constraint(x, pltpu.HBM) for x in (green, coupling, coulomb)))
        return tuple(
            pl.pallas_call(
                store,
                out_shape=shapes,
                in_specs=[near] * 2,
                out_specs=[far] * 2,
                scratch_shapes=[pltpu.SemaphoreType.DMA((2,))],
                compiler_params=pltpu.CompilerParams(vmem_limit_bytes=8 * 1024 * 1024),
                name="store",
            )(*held)
        )

    placed = (P("energy", "slab", None, None), P("slab", None, None), P("slab", None, None))
    return jax.shard_map(
        step,
        mesh=mesh,
        in_specs=placed,
        out_specs=(P("energy", "slab", None, None),) * 2,
        check_vma=False,
    )
```

time: 58.6 us -> 57.5 us (0.981); the launches traced: 58.5 us -> 56.6 us
  Pallas kernels: 57.8 us -> 56 us
    pallas_call x1, Pallas kernels: 56.5 us -> 54.6 us  [step(): pl.pallas_call(functools.partial(kernel, n, ns, sizes), out_shape=shapes,...]
where the time goes in v1:
time: 57.5 us; the launch traced here: 56.6 us
  Pallas kernels  56 us (97%)
  between operations  0.64 us (1%)
    pallas_call x1, Pallas kernels, step(): pl.pallas_call(functools.partial(kernel, n, ns, sizes), out_shape=shapes,...  54.6 us
    pallas_call x1, Pallas kernels, step(): pl.pallas_call(store, out_shape=shapes, in_specs=[near] * 2, out_specs=[f...  1.33 us

profile of v1, /device:TPU:1, one launch (start us, length us, event | category | flops | bytes accessed | tf_op | source)
XLA Modules:
  0.0 56.6 jit_solution(12877432442827631151)
XLA Ops:
  0.6 54.6 %step.1 = (bf16[2,1,512,512]{3,2,1,0:T(8,128)(2,1)S(1)}, bf16[2,1,512,512]{3,2,1,0:T(8,128)(2,1)S(1)}) custom-call(bf16[2,1,512,512]{3,2,1,0:T(8,128)(2,1)} %green.1, bf16[1,512,512]{2,1,0:T(8,128)(2,1)} %coupling.1, bf16[1,512,512]{2,1,0:T(8,128)(2,1)} %coulomb.1), custom_call_target="tpu_custom_call" | custom-call | tf_op jit(solution)/shard_map/step/pallas_call | solution.py:370
  55.3 1.3 %store.1 = (bf16[2,1,512,512]{3,2,1,0:T(8,128)(2,1)}, bf16[2,1,512,512]{3,2,1,0:T(8,128)(2,1)}) custom-call(bf16[2,1,512,512]{3,2,1,0:T(8,128)(2,1)S(1)} %get-tuple-element.4.sigma, bf16[2,1,512,512]{3,2,1,0:T(8,128)(2,1)S(1)} %get-tuple-element.5.screen), custom_call_target="tpu_custom_call" | custom-call | tf_op jit(solution)/shard_map/store/pallas_call | solution.py:388

commit v2 on v1

--- a/solution.py
+++ b/solution.py
@@ -60,17 +60,14 @@
 
 
 def split(rows):
-    units, sizes = rows // TILE, []
-    while units > 1 and len(sizes) < 1:
-        sizes.append(units - units // 2)
-        units //= 2
-    return [size * TILE for size in sizes + [units]]
+    units = rows // TILE
+    return [size * TILE for size in (units - units // 2, units // 2) if size]
 
 
 def kernel(
     n, ns, sizes, green, coupling, coulomb, sigma, screen,
     g, h, c, gath, prow, pol, inner, rim_b, rim_a, g_above, low_in, low_out, outer,
-    local, ss1, rs1, ss2, rs2, ssb, rsb, ssa, rsa, sside, rside, seen,
+    local, ss1, rs1, ss2, rs2, ssr, rsb, rsa, sside, rside, seen,
 ):
     per, m = g.shape[0], g.shape[1]
     parts, last = range(len(sizes)), len(sizes) - 1
@@ -80,24 +77,33 @@
     has_up, has_down = slab < ns - 1, slab > 0
     long = n // 2
     half = max(long // 2, 1)
+    width = 2 * half
     z, y = me // 2, me % 2
     low = z < half
     base = jnp.where(low, 0, half)
-
-    def pair(place):
-        return [place * 2 + y, place * 2 + 1 - y]
+    edge = jnp.where(low, z, long - 1 - z)
+
+    def across(k):
+        return jnp.where(low, long - 1 - k, k)
 
     near = [me + 1 - 2 * y]
     for k in range(1, half):
-        near += pair(base + (z - base + k) % half)
+        place = base + (z - base + k) % half
+        near += [place * 2 + y, place * 2 + 1 - y]
     cross = []
     for k in range(long - half):
-        cross += pair(jnp.where(low, long - 1 - k, k))
+        cross += [across(k) * 2 + y, across(k) * 2 + 1 - y]
     others = near + cross
 
+    inside = (base * 2, width, 0)
+    far = [(across(k) * 2, 2, 1 + k) for k in range(long - half - 1)]
+    facing = [(cross[-2], 1, half), (cross[-1], 1, half + 1)] if cross else []
+
+    def rows_of(part, first, count):
+        return pl.ds(pl.multiple_of(n * starts[part] + first * sizes[part], TILE), count * sizes[part])
+
     def block(part, owner):
-        rows = sizes[part]
-        return pl.ds(pl.multiple_of(n * starts[part] + owner * rows, TILE), rows)
+        return rows_of(part, owner, 1)
 
     def strip(part):
         return pl.ds(starts[part], sizes[part])
@@ -118,8 +124,7 @@
         )
         for part in parts
     ]
-    for copy in loads + own:
-        copy.start()
+    loads[0].start()
 
     def remote(src, dst, send, recv, where):
         return pltpu.make_async_remote_copy(
@@ -136,9 +141,9 @@
         found += [(steps, 1) for steps in sorted({distance - 1, 1 - distance}, reverse=True)]
         return [at(*place) for place in found]
 
-    def greet(sem, others):
+    def greet(sem, friends):
         count = jnp.int32(0)
-        for where, there in others:
+        for where, there in friends:
             @pl.when(there)
             def _():
                 pl.semaphore_signal(sem, inc=1, device_id=where, device_id_type=MESH)
@@ -150,15 +155,12 @@
         return remote(
             g.at[:, block(part, to)],
             gath.at[pl.ds(me * per, per), strip(part)],
-            ss1.at[part, to], rs1.at[part, me], {"energy": to},
+            ss1.at[part], rs1.at[part], {"energy": to},
         )
 
-    def gathered(part, other):
-        return remote(
-            g.at[:, block(part, other)],
-            gath.at[pl.ds(other * per, per), strip(part)],
-            ss1.at[part, other], rs1.at[part, other], {"energy": other},
-        )
+    def gathered(part):
+        pieces = gath.at[pl.ds(0, (n - 1) * per), strip(part)]
+        return remote(pieces, pieces, ss1.at[part], rs1.at[part], {"energy": near[0]})
 
     beside = [({"energy": to}, there) for to, there in ring(1)]
     for distance in range(1, long + 1):
@@ -172,6 +174,8 @@
             def _():
                 gather(0, to).start()
 
+    for copy in own + loads[1:]:
+        copy.start()
     for part in parts[1:]:
         for to in others:
             gather(part, to).start()
@@ -223,121 +227,151 @@
 
         lax.fori_loop(0, per, upper, 0)
 
-    def scatter(part, to):
+    def scatter(part, to, sem):
         return remote(
             prow.at[pl.ds(to * per, per), strip(part)], pol.at[:, block(part, me)],
-            ss2.at[part, to], rs2.at[part, me], {"energy": to},
+            ss2.at[part], rs2.at[part, sem], {"energy": to},
         )
 
-    def scattered(part, other):
-        return remote(
-            prow.at[pl.ds(other * per, per), strip(part)], pol.at[:, block(part, other)],
-            ss2.at[part, other], rs2.at[part, other], {"energy": other},
-        )
-
-    def to_up(part, owner):
-        piece = block(part, owner)
-        return remote(pol.at[:, piece], rim_b.at[:, piece], ssb.at[part, owner], rsb.at[part, owner], {"slab": up})
-
-    def to_down(part, owner):
-        piece = block(part, owner)
-        return remote(pol.at[:, piece], rim_a.at[:, piece], ssa.at[part, owner], rsa.at[part, owner], {"slab": down})
-
-    def forward(part, owner):
+    def scatter_near(part):
+        for to in near:
+            scatter(part, to, 0).start()
+
+    def scatter_cross(part):
+        queue = list(enumerate(cross))
+        for i, to in queue[:-2] + queue[:-3:-1]:
+            scatter(part, to, 1 + edge + (edge == half - 1).astype(jnp.int32) * (i % 2)).start()
+
+    def scattered(part, group):
+        first, count, sem = group
+        count = width - 1 if sem == 0 else count
+        rows = pl.ds(n * starts[part], count * sizes[part])
+        return remote(pol.at[:, rows], pol.at[:, rows], ss2.at[part], rs2.at[part, sem], {"energy": near[0]})
+
+    def to_up(part, group):
+        rows = rows_of(part, *group[:2])
+        return remote(pol.at[:, rows], rim_b.at[:, rows], ssr.at[0], rsb.at[part, group[2]], {"slab": up})
+
+    def to_down(part, group):
+        rows = rows_of(part, *group[:2])
+        return remote(pol.at[:, rows], rim_a.at[:, rows], ssr.at[1], rsa.at[part, group[2]], {"slab": down})
+
+    def forward(part, group):
+        scattered(part, group).wait_recv()
+
         @pl.when(has_up)
         def _():
-            to_up(part, owner).start()
+            to_up(part, group).start()
 
         @pl.when(has_down)
         def _():
-            to_down(part, owner).start()
-
-    def arrive(part, owner):
+            to_down(part, group).start()
+
+    def arrive(part, group):
         @pl.when(has_down)
         def _():
-            to_up(part, owner).wait_recv()
+            to_up(part, group).wait_recv()
 
         @pl.when(has_up)
         def _():
-            to_down(part, owner).wait_recv()
-
-    def depart(part):
-        @pl.when(has_up)
-        def _():
-            for owner in [me] + others:
-                to_up(part, owner).wait_send()
-
-        @pl.when(has_down)
-        def _():
-            for owner in [me] + others:
-                to_down(part, owner).wait_send()
-
-    def finish(piece):
+            to_down(part, group).wait_recv()
+
+    def finish(rows):
         for e in range(per):
-            sides = rim_b[e, piece].astype(F32) + rim_a[e, piece].astype(F32)
-            screen[e, 0, piece] = (outer[e, piece] + 0.5 * sides).astype(BF16)
-
-    def screened(rows, first):
-        def product(e, _):
-            inner[e, rows] = matmul(pol[e, rows], c[...], 1, 1).astype(BF16)
-            term = matmul(c[:, rows], inner[e, rows])
-            outer[e] = term if first else outer[e] + term
-            return 0
-
-        lax.fori_loop(0, per, product, 0)
+            sides = rim_b[e, rows].astype(F32) + rim_a[e, rows].astype(F32)
+            screen[e, 0, rows] = (outer[e, rows] + 0.5 * sides).astype(BF16)
+
+    def screened(rows, fresh):
+        both = matmul(pol[:, rows].reshape(per * rows.size, m), c[...], 1, 1).astype(BF16)
+        for e in range(per):
+            term = matmul(c[:, rows], both[e * rows.size : (e + 1) * rows.size])
+            outer[e] = term if fresh else outer[e] + term
+
+    def side(part, opposite):
+        count = width * sizes[part]
+        first = jnp.where(low, 0, count)
+        offset = count - first if opposite else first
+        return pl.ds(pl.multiple_of(n * starts[part] + offset, LANES), count)
+
+    cut = n > 2 and all(width * size % LANES == 0 for size in sizes)
+
+    late = (edge > 0) & ((slab == 0) | (slab == ns - 1)) if last else edge < 0
 
     for part in parts:
         own[part].wait()
-        for other in others:
-            gathered(part, other).wait_recv()
+        gathered(part).wait_recv()
+        if part:
+            @pl.when(edge == 0)
+            def _():
+                scatter_cross(part - 1)
+
         correlate(gath, prow, starts[part], sizes[part])
-        for to in others:
-            scatter(part, to).start()
+        scatter_near(part)
+        if part < last:
+            @pl.when(edge > 0)
+            def _():
+                scatter_cross(part)
+        else:
+            @pl.when(jnp.logical_not(late))
+            def _():
+                scatter_cross(part)
+
         pol[:, block(part, me)] = prow[pl.ds(me * per, per), strip(part)]
-        forward(part, me)
         if part == 0:
             self_energy()
 
     loads[2].wait()
     for part in parts:
-        count = long * sizes[part]
-        cut = part == last and n > 2 and n * starts[part] % LANES == count % LANES == 0
-        for other in near:
-            scattered(part, other).wait_recv()
-            forward(part, other)
+        forward(part, inside)
         if cut:
-            side = jnp.where(low, 0, count)
-            screened(pl.ds(pl.multiple_of(n * starts[part] + side, LANES), count), part == 0)
-        for other in cross:
-            scattered(part, other).wait_recv()
-            forward(part, other)
+            screened(side(part, False), part == 0)
+        if part < last:
+            for group in far:
+                forward(part, group)
+    for part in parts:
+        gathered(part).wait_send()
+    for part in parts:
+        if part == last:
+            for group in far:
+                forward(part, group)
+        for group in facing:
+            forward(part, group)
         if cut:
-            screened(pl.ds(pl.multiple_of(n * starts[part] + count - side, LANES), count), False)
+            screened(side(part, True), False)
         else:
             screened(span(part), part == 0)
+        if part == last - 1:
+            @pl.when(late)
+            def _():
+                scatter_cross(last)
+
 
     for part in parts[:last]:
-        for owner in [me] + others:
-            arrive(part, owner)
+        for group in [inside] + far + facing:
+            arrive(part, group)
         finish(span(part))
-        depart(part)
+    for group in [inside] + far:
+        arrive(last, group)
+        finish(rows_of(last, *group[:2]))
+
     for part in parts:
-        for other in others:
-            gathered(part, other).wait_send()
-            scattered(part, other).wait_send()
+        remote(
+            gath.at[pl.ds(0, (n - 1) * per), strip(part)], gath.at[pl.ds(0, (n - 1) * per), strip(part)],
+            ss2.at[part], rs1.at[part], {"energy": near[0]},
+        ).wait_send()
+    for group in facing:
+        arrive(last, group)
+        finish(rows_of(last, *group[:2]))
 
     @pl.when(has_up)
     def _():
         lower_up.wait_send()
+        remote(pol, rim_b, ssr.at[0], rsb.at[0, 0], {"slab": up}).wait_send()
 
     @pl.when(has_down)
     def _():
         green_down.wait_send()
-
-    for owner in [me] + others:
-        arrive(last, owner)
-        finish(block(last, owner))
-    depart(last)
+        remote(pol, rim_a, ssr.at[1], rsa.at[0, 0], {"slab": down}).wait_send()
 
 
 def store(sigma, screen, sigma_out, screen_out, sems):
@@ -363,7 +397,9 @@
         blocks = pltpu.VMEM((per, m, m), BF16)
         square = pltpu.VMEM((m, m), BF16)
         strip = pltpu.VMEM((count, rows, m), BF16)
-        sems = pltpu.SemaphoreType.DMA((parts, n))
+        groups = pltpu.SemaphoreType.DMA((parts, max(n // 4, 1) + 2))
+        one = pltpu.SemaphoreType.DMA((parts,))
+        two = pltpu.SemaphoreType.DMA((2,))
         shapes = [jax.ShapeDtypeStruct(green.shape, BF16)] * 2
         near = pl.BlockSpec(memory_space=pltpu.VMEM)
         far = pl.BlockSpec(memory_space=pltpu.HBM)
@@ -376,8 +412,7 @@
             + [blocks] * 6
             + [blocks, pltpu.VMEM((per, m, m), F32)]
             + [pltpu.SemaphoreType.DMA((3 + parts,))]
-            + [sems] * 8
-            + [pltpu.SemaphoreType.DMA((2,))] * 2
+            + [one, one, one, groups, two, groups, groups, two, two]
             + [pltpu.SemaphoreType.REGULAR((max(n // 2 - 1, 1),))],
             compiler_params=pltpu.CompilerParams(
                 collective_id=0, has_side_effects=True, vmem_limit_bytes=40 * 1024 * 1024

time: 57.5 us -> 54.8 us (0.953)
  Pallas kernels: 56 us -> 53.7 us
    pallas_call x1, Pallas kernels: 54.6 us -> 52.4 us  [step(): pl.pallas_call(functools.partial(kernel, n, ns, sizes), out_shape=shapes,...]
where the time goes in v2:
time: 54.8 us; the launch traced here: 54.3 us
  Pallas kernels  53.7 us (98%)
  between operations  0.64 us (1%)
    pallas_call x1, Pallas kernels, step(): pl.pallas_call(functools.partial(kernel, n, ns, sizes), out_shape=shapes,...  52.4 us
    pallas_call x1, Pallas kernels, step(): pl.pallas_call(store, out_shape=shapes, in_specs=[near] * 2, out_specs=[f...  1.33 us

profile of v2, /device:TPU:1, one launch (start us, length us, event | category | flops | bytes accessed | tf_op | source)
XLA Modules:
  0.0 54.3 jit_solution(1471252926431454773)
XLA Ops:
  0.6 52.4 %step.1 = (bf16[2,1,512,512]{3,2,1,0:T(8,128)(2,1)S(1)}, bf16[2,1,512,512]{3,2,1,0:T(8,128)(2,1)S(1)}) custom-call(bf16[2,1,512,512]{3,2,1,0:T(8,128)(2,1)} %green.1, bf16[1,512,512]{2,1,0:T(8,128)(2,1)} %coupling.1, bf16[1,512,512]{2,1,0:T(8,128)(2,1)} %coulomb.1), custom_call_target="tpu_custom_call" | custom-call | tf_op jit(solution)/shard_map/step/pallas_call | solution.py:406
  53.0 1.3 %store.1 = (bf16[2,1,512,512]{3,2,1,0:T(8,128)(2,1)}, bf16[2,1,512,512]{3,2,1,0:T(8,128)(2,1)}) custom-call(bf16[2,1,512,512]{3,2,1,0:T(8,128)(2,1)S(1)} %get-tuple-element.4.sigma, bf16[2,1,512,512]{3,2,1,0:T(8,128)(2,1)S(1)} %get-tuple-element.5.screen), custom_call_target="tpu_custom_call" | custom-call | tf_op jit(solution)/shard_map/store/pallas_call | solution.py:423

commit v3 on v2

--- a/solution.py
+++ b/solution.py
@@ -97,7 +97,8 @@
 
     inside = (base * 2, width, 0)
     far = [(across(k) * 2, 2, 1 + k) for k in range(long - half - 1)]
-    facing = [(cross[-2], 1, half), (cross[-1], 1, half + 1)] if cross else []
+    swap = (edge == half - 1).astype(jnp.int32)
+    facing = [(across(long - half - 1) * 2 + (y + k) % 2, 1, half + k) for k in (swap, 1 - swap)] if cross else []
 
     def rows_of(part, first, count):
         return pl.ds(pl.multiple_of(n * starts[part] + first * sizes[part], TILE), count * sizes[part])
@@ -239,12 +240,12 @@
 
     def scatter_cross(part):
         queue = list(enumerate(cross))
-        for i, to in queue[:-2] + queue[:-3:-1]:
+        for i, to in [queue[k ^ 1] for k in range(len(queue))]:
             scatter(part, to, 1 + edge + (edge == half - 1).astype(jnp.int32) * (i % 2)).start()
 
     def scattered(part, group):
         first, count, sem = group
-        count = width - 1 if sem == 0 else count
+        count = width - 1 if group is inside else count
         rows = pl.ds(n * starts[part], count * sizes[part])
         return remote(pol.at[:, rows], pol.at[:, rows], ss2.at[part], rs2.at[part, sem], {"energy": near[0]})
 
@@ -325,15 +326,11 @@
         forward(part, inside)
         if cut:
             screened(side(part, False), part == 0)
-        if part < last:
-            for group in far:
-                forward(part, group)
+        for group in far:
+            forward(part, group)
     for part in parts:
         gathered(part).wait_send()
     for part in parts:
-        if part == last:
-            for group in far:
-                forward(part, group)
         for group in facing:
             forward(part, group)
         if cut:

time: 54.8 us -> 54.1 us (0.987)
  Pallas kernels: 53.7 us -> 53 us
    pallas_call x1, Pallas kernels: 52.4 us -> 51.7 us  [step(): pl.pallas_call(functools.partial(kernel, n, ns, sizes), out_shape=shapes,...]
where the time goes in v3:
time: 54.1 us; the launch traced here: 53.6 us
  Pallas kernels  53 us (98%)
  between operations  0.64 us (1%)
    pallas_call x1, Pallas kernels, step(): pl.pallas_call(functools.partial(kernel, n, ns, sizes), out_shape=shapes,...  51.7 us
    pallas_call x1, Pallas kernels, step(): pl.pallas_call(store, out_shape=shapes, in_specs=[near] * 2, out_specs=[f...  1.33 us

profile of v3, /device:TPU:1, one launch (start us, length us, event | category | flops | bytes accessed | tf_op | source)
XLA Modules:
  0.0 53.6 jit_solution(12478134292336828762)
XLA Ops:
  0.6 51.7 %step.1 = (bf16[2,1,512,512]{3,2,1,0:T(8,128)(2,1)S(1)}, bf16[2,1,512,512]{3,2,1,0:T(8,128)(2,1)S(1)}) custom-call(bf16[2,1,512,512]{3,2,1,0:T(8,128)(2,1)} %green.1, bf16[1,512,512]{2,1,0:T(8,128)(2,1)} %coupling.1, bf16[1,512,512]{2,1,0:T(8,128)(2,1)} %coulomb.1), custom_call_target="tpu_custom_call" | custom-call | tf_op jit(solution)/shard_map/step/pallas_call | solution.py:403
  52.3 1.3 %store.1 = (bf16[2,1,512,512]{3,2,1,0:T(8,128)(2,1)}, bf16[2,1,512,512]{3,2,1,0:T(8,128)(2,1)}) custom-call(bf16[2,1,512,512]{3,2,1,0:T(8,128)(2,1)S(1)} %get-tuple-element.4.sigma, bf16[2,1,512,512]{3,2,1,0:T(8,128)(2,1)S(1)} %get-tuple-element.5.screen), custom_call_target="tpu_custom_call" | custom-call | tf_op jit(solution)/shard_map/store/pallas_call | solution.py:420

commit v4 on v3

--- a/solution.py
+++ b/solution.py
@@ -97,8 +97,7 @@
 
     inside = (base * 2, width, 0)
     far = [(across(k) * 2, 2, 1 + k) for k in range(long - half - 1)]
-    swap = (edge == half - 1).astype(jnp.int32)
-    facing = [(across(long - half - 1) * 2 + (y + k) % 2, 1, half + k) for k in (swap, 1 - swap)] if cross else []
+    facing = [(cross[-1], 1, half + 1), (cross[-2], 1, half)] if cross else []
 
     def rows_of(part, first, count):
         return pl.ds(pl.multiple_of(n * starts[part] + first * sizes[part], TILE), count * sizes[part])
@@ -142,16 +141,6 @@
         found += [(steps, 1) for steps in sorted({distance - 1, 1 - distance}, reverse=True)]
         return [at(*place) for place in found]
 
-    def greet(sem, friends):
-        count = jnp.int32(0)
-        for where, there in friends:
-            @pl.when(there)
-            def _():
-                pl.semaphore_signal(sem, inc=1, device_id=where, device_id_type=MESH)
-
-            count = count + there.astype(jnp.int32)
-        pl.semaphore_wait(sem, count)
-
     def gather(part, to):
         return remote(
             g.at[:, block(part, to)],
@@ -163,23 +152,62 @@
         pieces = gath.at[pl.ds(0, (n - 1) * per), strip(part)]
         return remote(pieces, pieces, ss1.at[part], rs1.at[part], {"energy": near[0]})
 
+    def tell(sem, friends):
+        for where, there in friends:
+            @pl.when(there)
+            def _():
+                pl.semaphore_signal(sem, inc=1, device_id=where, device_id_type=MESH)
+
+    def hear(sem, friends):
+        pl.semaphore_wait(sem, sum(there.astype(jnp.int32) for _, there in friends))
+
+    def send(pairs):
+        for to, there in pairs:
+            @pl.when(there)
+            def _():
+                gather(0, to).start()
+
+    inward, _ = at(jnp.where(low, 1, -1), 0)
+    outward, _ = at(jnp.where(low, -1, 1), 0)
+    flip = near[0]
+    anyone = me >= 0
+    opposite = (edge == half - 1) & (long > 1)
+    deeper, outer_one = (edge < half - 1) & (long > 1), edge > 0
+    by_slab = [({"slab": up}, has_up), ({"slab": down}, has_down)]
+    by_side = [({"energy": flip}, anyone), ({"energy": inward}, opposite)]
+    barrier = pltpu.get_barrier_semaphore()
+    tell(barrier, by_side + [({"energy": outward}, outer_one)] + by_slab)
+    hear(barrier, by_side + [({"energy": inward}, deeper)] + by_slab)
+    loads[0].wait()
+    send([(inward, opposite | deeper), (flip, anyone)])
+    if cross:
+        @pl.when(edge == half - 1)
+        def _():
+            for part in parts[1:]:
+                gather(part, cross[-2]).start()
+
+    tell(seen.at[0], [({"energy": inward}, deeper)])
+
+    @pl.when(outer_one)
+    def _():
+        pl.semaphore_wait(seen.at[0], 1)
+
+    send([(outward, outer_one)])
+
     beside = [({"energy": to}, there) for to, there in ring(1)]
-    for distance in range(1, long + 1):
-        if distance == 1:
-            greet(pltpu.get_barrier_semaphore(), beside + [({"slab": up}, has_up), ({"slab": down}, has_down)])
-            loads[0].wait()
-        else:
-            greet(seen.at[distance - 2], beside)
-        for to, there in ring(distance):
-            @pl.when(there)
-            def _():
-                gather(0, to).start()
+    for distance in range(2, long + 1):
+        tell(seen.at[distance - 1], beside)
+        hear(seen.at[distance - 1], beside)
+        send(ring(distance))
 
     for copy in own + loads[1:]:
         copy.start()
     for part in parts[1:]:
-        for to in others:
-            gather(part, to).start()
+        for i, to in enumerate(others):
+            @pl.when((edge < half - 1) | (i != n - 3))
+            def _():
+                gather(part, to).start()
+
 
     green_down = remote(g, g_above, sside.at[0], rside.at[0], {"slab": down})
     lower_up = remote(low_out, low_in, sside.at[1], rside.at[1], {"slab": up})
@@ -296,7 +324,7 @@
 
     cut = n > 2 and all(width * size % LANES == 0 for size in sizes)
 
-    late = (edge > 0) & ((slab == 0) | (slab == ns - 1)) if last else edge < 0
+    late = (edge > 0) & (slab == ns - 1) if last else edge < 0
 
     for part in parts:
         own[part].wait()
@@ -340,12 +368,20 @@
         if part == last - 1:
             @pl.when(late)
             def _():
+                for group in facing:
+                    to_up(part, group).wait_recv()
                 scatter_cross(last)
 
 
     for part in parts[:last]:
-        for group in [inside] + far + facing:
+        for group in [inside] + far:
             arrive(part, group)
+
+        @pl.when(jnp.logical_not(late))
+        def _():
+            for group in facing:
+                arrive(part, group)
+
         finish(span(part))
     for group in [inside] + far:
         arrive(last, group)
@@ -410,7 +446,7 @@
             + [blocks, pltpu.VMEM((per, m, m), F32)]
             + [pltpu.SemaphoreType.DMA((3 + parts,))]
             + [one, one, one, groups, two, groups, groups, two, two]
-            + [pltpu.SemaphoreType.REGULAR((max(n // 2 - 1, 1),))],
+            + [pltpu.SemaphoreType.REGULAR((n // 2,))],
             compiler_params=pltpu.CompilerParams(
                 collective_id=0, has_side_effects=True, vmem_limit_bytes=40 * 1024 * 1024
             ),

time: 54.1 us -> 53.9 us (level)
  no operation moved by 1% of the time
where the time goes in v4:
time: 53.9 us; the launch traced here: 53.2 us
  Pallas kernels  52.5 us (97%)
  between operations  0.64 us (1%)
    pallas_call x1, Pallas kernels, step(): pl.pallas_call(functools.partial(kernel, n, ns, sizes), out_shape=shapes,...  51.2 us
    pallas_call x1, Pallas kernels, step(): pl.pallas_call(store, out_shape=shapes, in_specs=[near] * 2, out_specs=[f...  1.33 us

profile of v4, /device:TPU:1, one launch (start us, length us, event | category | flops | bytes accessed | tf_op | source)
XLA Modules:
  0.0 53.2 jit_solution(7428966675641508536)
XLA Ops:
  0.6 51.2 %step.1 = (bf16[2,1,512,512]{3,2,1,0:T(8,128)(2,1)S(1)}, bf16[2,1,512,512]{3,2,1,0:T(8,128)(2,1)S(1)}) custom-call(bf16[2,1,512,512]{3,2,1,0:T(8,128)(2,1)} %green.1, bf16[1,512,512]{2,1,0:T(8,128)(2,1)} %coupling.1, bf16[1,512,512]{2,1,0:T(8,128)(2,1)} %coulomb.1), custom_call_target="tpu_custom_call" | custom-call | tf_op jit(solution)/shard_map/step/pallas_call | solution.py:439
  51.8 1.3 %store.1 = (bf16[2,1,512,512]{3,2,1,0:T(8,128)(2,1)}, bf16[2,1,512,512]{3,2,1,0:T(8,128)(2,1)}) custom-call(bf16[2,1,512,512]{3,2,1,0:T(8,128)(2,1)S(1)} %get-tuple-element.4.sigma, bf16[2,1,512,512]{3,2,1,0:T(8,128)(2,1)S(1)} %get-tuple-element.5.screen), custom_call_target="tpu_custom_call" | custom-call | tf_op jit(solution)/shard_map/store/pallas_call | solution.py:456

commit v5 on v3

--- a/solution.py
+++ b/solution.py
@@ -97,8 +97,7 @@
 
     inside = (base * 2, width, 0)
     far = [(across(k) * 2, 2, 1 + k) for k in range(long - half - 1)]
-    swap = (edge == half - 1).astype(jnp.int32)
-    facing = [(across(long - half - 1) * 2 + (y + k) % 2, 1, half + k) for k in (swap, 1 - swap)] if cross else []
+    facing = [(cross[-1], 1, half + 1), (cross[-2], 1, half)] if cross else []
 
     def rows_of(part, first, count):
         return pl.ds(pl.multiple_of(n * starts[part] + first * sizes[part], TILE), count * sizes[part])
@@ -296,7 +295,7 @@
 
     cut = n > 2 and all(width * size % LANES == 0 for size in sizes)
 
-    late = (edge > 0) & ((slab == 0) | (slab == ns - 1)) if last else edge < 0
+    late = (edge > 0) & (slab == ns - 1) if last else edge < 0
 
     for part in parts:
         own[part].wait()
@@ -340,12 +339,20 @@
         if part == last - 1:
             @pl.when(late)
             def _():
+                for group in facing:
+                    to_up(part, group).wait_recv()
                 scatter_cross(last)
 
 
     for part in parts[:last]:
-        for group in [inside] + far + facing:
+        for group in [inside] + far:
             arrive(part, group)
+
+        @pl.when(jnp.logical_not(late))
+        def _():
+            for group in facing:
+                arrive(part, group)
+
         finish(span(part))
     for group in [inside] + far:
         arrive(last, group)

time: 54.1 us -> 53.8 us (level)
  no operation moved by 1% of the time
where the time goes in v5:
time: 53.8 us; the launch traced here: 53.7 us
  Pallas kernels  53 us (99%)
  between operations  0.64 us (1%)
    pallas_call x1, Pallas kernels, step(): pl.pallas_call(functools.partial(kernel, n, ns, sizes), out_shape=shapes,...  51.7 us
    pallas_call x1, Pallas kernels, step(): pl.pallas_call(store, out_shape=shapes, in_specs=[near] * 2, out_specs=[f...  1.33 us

profile of v5, /device:TPU:1, one launch (start us, length us, event | category | flops | bytes accessed | tf_op | source)
XLA Modules:
  0.0 53.7 jit_solution(7478930737250603306)
XLA Ops:
  0.6 51.7 %step.1 = (bf16[2,1,512,512]{3,2,1,0:T(8,128)(2,1)S(1)}, bf16[2,1,512,512]{3,2,1,0:T(8,128)(2,1)S(1)}) custom-call(bf16[2,1,512,512]{3,2,1,0:T(8,128)(2,1)} %green.1, bf16[1,512,512]{2,1,0:T(8,128)(2,1)} %coupling.1, bf16[1,512,512]{2,1,0:T(8,128)(2,1)} %coulomb.1), custom_call_target="tpu_custom_call" | custom-call | tf_op jit(solution)/shard_map/step/pallas_call | solution.py:410
  52.3 1.3 %store.1 = (bf16[2,1,512,512]{3,2,1,0:T(8,128)(2,1)}, bf16[2,1,512,512]{3,2,1,0:T(8,128)(2,1)}) custom-call(bf16[2,1,512,512]{3,2,1,0:T(8,128)(2,1)S(1)} %get-tuple-element.4.sigma, bf16[2,1,512,512]{3,2,1,0:T(8,128)(2,1)S(1)} %get-tuple-element.5.screen), custom_call_target="tpu_custom_call" | custom-call | tf_op jit(solution)/shard_map/store/pallas_call | solution.py:427
